TPU v7x, 32 devices: a whole 2x2x4 slice. The times are simulated.
32 devices in a mesh: gx: 4 (over z), gy: 8 (over y, x, core).
Axes of the slice: x: 2, y: 2, z: 4, core: 2. Of those that a mesh axis runs over, the one named last changes fastest.
Arguments:
- probes: float32 [8, 64, 128, 512], P(None, 'gx', 'gy'), may hold values from -12.5 to 12.5, as said below
- disorder: float32 [64, 128, 512], P('gx', 'gy'), may hold values from -2 to 2
- spectrum_center: float32 [1], replicated, may hold values from -0.5 to 0.5
- half_width: float32 [1], replicated, may hold values from 9 to 11
Outputs:
- last_vector: float32 [8, 64, 128, 512], P(None, 'gx', 'gy')
- moments: float32 [8, 8], replicated
Inputs may be any that keep to these rules, and one draw needn't show every extreme that they name: `probes`: real-valued probe entries.
All inputs are finite; a program needn't handle non-finite values.
Results may differ from a plain program's by a relative error of at most 0.0001.
Values sent between devices are 32-bit elements; how exact they have to be, the bound alone decides.
A program may use at most 128 MiB of HBM per device.

v0:
```python
import functools

import jax
import jax.numpy as jnp
from jax import lax
from jax.experimental import pallas as pl
from jax.experimental.pallas import tpu as pltpu
from jax.sharding import PartitionSpec as P

STEPS = 4
MESH = pl.DeviceIdType.MESH
ROWS = 8


def kernel(counts, sites, probes_hbm, disorder_hbm, center, width, last, moments, *scratch):
    fields = scratch[:STEPS]
    (disorder, near, faces, coef, acc, gather_x, gather_y, load_sem, energy_sem, send_sem, recv_sem,
     xs_sem, xr_sem, ys_sem, yr_sem) = scratch[STEPS:]
    n_probes, nx, ny, nz = probes_hbm.shape
    tiles = ny // ROWS
    count_x, count_y = counts
    me_x = lax.axis_index("gx")
    me_y = lax.axis_index("gy")

    def at_x(offset):
        return (lax.rem(me_x + offset, count_x), me_y)

    def at_y(offset):
        return (me_x, lax.rem(me_y + offset, count_y))

    def load(p):
        return pltpu.make_async_copy(
            probes_hbm.at[p], fields[0].at[p, pl.ds(1, nx)], load_sem.at[p])

    def x_sends(s, p):
        if s == 0:
            low, high = probes_hbm.at[p, 0], probes_hbm.at[p, nx - 1]
        else:
            low, high = fields[s].at[p, 1], fields[s].at[p, nx]
        return (
            pltpu.make_async_remote_copy(
                low, fields[s].at[p, nx + 1], send_sem.at[s, p, 0], recv_sem.at[s, p, 0],
                device_id=at_x(count_x - 1), device_id_type=MESH),
            pltpu.make_async_remote_copy(
                high, fields[s].at[p, 0], send_sem.at[s, p, 1], recv_sem.at[s, p, 1],
                device_id=at_x(1), device_id_type=MESH),
        )

    def y_sends(s, p):
        return (
            pltpu.make_async_remote_copy(
                faces.at[s, 0, p], near.at[s, 1, p], send_sem.at[s, p, 2], recv_sem.at[s, p, 2],
                device_id=at_y(count_y - 1), device_id_type=MESH),
            pltpu.make_async_remote_copy(
                faces.at[s, 1, p], near.at[s, 0, p], send_sem.at[s, p, 3], recv_sem.at[s, p, 3],
                device_id=at_y(1), device_id_type=MESH),
        )

    barrier = pltpu.get_barrier_semaphore()
    for offset in range(1, count_x):
        pl.semaphore_signal(barrier, inc=1, device_id=at_x(offset), device_id_type=MESH)
    for offset in range(1, count_y):
        pl.semaphore_signal(barrier, inc=1, device_id=at_y(offset), device_id_type=MESH)

    @pl.loop(0, n_probes)
    def _(p):
        load(p).start()

    energy = pltpu.make_async_copy(disorder_hbm, disorder, energy_sem)
    energy.start()
    scale = 2.0 / jnp.full((ROWS, nz), width[0], jnp.float32)
    middle = center[0]

    pl.semaphore_wait(barrier, count_x + count_y - 2)

    @pl.loop(0, n_probes)
    def _(p):
        for copy in x_sends(0, p):
            copy.start()

    @pl.loop(0, n_probes)
    def _(p):
        load(p).wait()

        @pl.loop(0, nx)
        def _(x):
            faces[0, 0, p, x] = fields[0][p, x + 1, pl.ds(0, 1)]
            faces[0, 1, p, x] = fields[0][p, x + 1, pl.ds(ny - 1, 1)]

        for copy in y_sends(0, p):
            copy.start()

    energy.wait()

    @pl.loop(0, nx)
    def _(x):
        for i in range(tiles):
            part = pl.ds(ROWS * i, ROWS)
            coef[x, part] = (disorder[x, part] - middle) * scale

    sub = lax.broadcasted_iota(jnp.int32, (ROWS, nz), 0)
    first = sub == 0
    final = sub == ROWS - 1
    lanes = lax.broadcasted_iota(jnp.int32, (n_probes, 128), 1)
    sums = jnp.zeros((n_probes, 128), jnp.float32)

    def fold(v):
        parts = [v[:, 128 * j:128 * (j + 1)] for j in range(nz // 128)]
        while len(parts) > 1:
            parts = [a + b for a, b in zip(parts[::2], parts[1::2])] + (
                [parts[-1]] if len(parts) % 2 else [])
        return parts[0]

    for s in range(STEPS):
        cur = fields[s]

        @pl.loop(0, n_probes)
        def _(p):
            for copy in x_sends(s, p) + y_sends(s, p):
                copy.wait_recv()

            def row(x, carry):
                square, cross = carry
                low = jnp.broadcast_to(near[s, 0, p, x], (ROWS, nz))
                high = jnp.broadcast_to(near[s, 1, p, x], (ROWS, nz))
                here = [cur[p, x + 1, pl.ds(ROWS * i, ROWS)] for i in range(tiles)]
                down = [pltpu.roll(v, 1, 0) for v in here]
                up = [pltpu.roll(v, ROWS - 1, 0) for v in here]
                for i in range(tiles):
                    part = pl.ds(ROWS * i, ROWS)
                    v = here[i]
                    below = jnp.where(first, low if i == 0 else down[i - 1], down[i])
                    above = jnp.where(final, high if i == tiles - 1 else up[i + 1], up[i])
                    beside = cur[p, x, part] + cur[p, x + 2, part]
                    beside = beside + (below + above)
                    beside = beside + (pltpu.roll(v, 1, 1) + pltpu.roll(v, nz - 1, 1))
                    new = coef[x, part] * v - scale * beside
                    if s == 0:
                        new = 0.5 * new
                    else:
                        new = new - fields[s - 1][p, x + 1, part]
                    if s + 1 < STEPS:
                        fields[s + 1][p, x + 1, part] = new
                        if i == 0:
                            faces[s + 1, 0, p, x] = new[0:1]
                        if i == tiles - 1:
                            faces[s + 1, 1, p, x] = new[ROWS - 1:ROWS]
                    else:
                        last[p, x, part] = new
                    square = square + fold(v * v)
                    cross = cross + fold(new * v)
                return square, cross

            zero = jnp.zeros((ROWS, 128), jnp.float32)
            square, cross = lax.fori_loop(0, nx, row, (zero, zero), unroll=16)
            acc[0, p] = square
            acc[1, p] = cross
            if s + 1 < STEPS:
                for copy in x_sends(s + 1, p) + y_sends(s + 1, p):
                    copy.start()
            for copy in x_sends(s, p) + y_sends(s, p):
                copy.wait_send()

        for k in range(2):
            total = jnp.sum(jnp.sum(acc[k], axis=1), axis=1, keepdims=True)
            sums = sums + jnp.where(lanes == 2 * s + k, total, 0.0)

    def reduce_over(value, gather, sends, recvs, me, count, where):
        gather[me] = value

        def send(offset):
            return pltpu.make_async_remote_copy(
                gather.at[me], gather.at[me], sends.at[offset], recvs.at[me],
                device_id=where(offset), device_id_type=MESH)

        for offset in range(1, count):
            send(offset).start()
        for offset in range(1, count):
            source = lax.rem(me + offset, count)
            pltpu.make_async_remote_copy(
                gather.at[source], gather.at[source], sends.at[offset], recvs.at[source],
                device_id=where(offset), device_id_type=MESH).wait_recv()
        total = gather[0]
        for k in range(1, count):
            total = total + gather[k]
        return total, send

    sums, send_x = reduce_over(sums, gather_x, xs_sem, xr_sem, me_x, count_x, at_x)
    sums, send_y = reduce_over(sums, gather_y, ys_sem, yr_sem, me_y, count_y, at_y)
    mean = sums / jnp.float32(sites)
    start = jnp.where(lax.rem(lanes, 2) == 0, mean[:, 0:1], mean[:, 1:2])
    moments[...] = (2.0 * mean - start)[:, :2 * STEPS]

    for offset in range(1, count_x):
        send_x(offset).wait_send()
    for offset in range(1, count_y):
        send_y(offset).wait_send()


def local(counts, probes, disorder, spectrum_center, half_width):
    n_probes, nx, ny, nz = probes.shape
    sites = nx * counts[0] * ny * counts[1] * nz
    f32 = jnp.float32
    dma = pltpu.SemaphoreType.DMA
    vmem = pl.BlockSpec(memory_space=pltpu.VMEM)
    hbm = pl.BlockSpec(memory_space=pl.ANY)
    smem = pl.BlockSpec(memory_space=pltpu.SMEM)
    return pl.pallas_call(
        functools.partial(kernel, counts, sites),
        out_shape=(
            pltpu.VMEM(probes.shape, f32),
            jax.ShapeDtypeStruct((n_probes, 2 * STEPS), f32),
        ),
        in_specs=[hbm, hbm, smem, smem],
        out_specs=(vmem, vmem),
        scratch_shapes=[pltpu.VMEM((n_probes, nx + 2, ny, nz), f32)] * STEPS + [
            pltpu.VMEM((nx, ny, nz), f32),
            pltpu.VMEM((STEPS, 2, n_probes, nx, 1, nz), f32),
            pltpu.VMEM((STEPS, 2, n_probes, nx, 1, nz), f32),
            pltpu.VMEM((nx, ny, nz), f32),
            pltpu.VMEM((2, n_probes, ROWS, 128), f32),
            pltpu.VMEM((counts[0], n_probes, 128), f32),
            pltpu.VMEM((counts[1], n_probes, 128), f32),
            dma((n_probes,)),
            dma,
            dma((STEPS, n_probes, 4)),
            dma((STEPS, n_probes, 4)),
            dma((counts[0],)),
            dma((counts[0],)),
            dma((counts[1],)),
            dma((counts[1],)),
        ],
        compiler_params=pltpu.CompilerParams(
            collective_id=0, has_side_effects=True, vmem_limit_bytes=46 * 1024 * 1024),
        name="moments",
    )(probes, disorder, spectrum_center, half_width)


def solution(mesh):
    counts = (mesh.shape["gx"], mesh.shape["gy"])
    in_specs = (P(None, "gx", "gy", None), P("gx", "gy", None), P(), P())
    out_specs = (P(None, "gx", "gy", None), P())
    return jax.shard_map(functools.partial(local, counts), mesh=mesh, in_specs=in_specs,
                         out_specs=out_specs, check_vma=False)
```

profile of v0, /device:TPU:0, one launch (start us, length us, event | category | flops | bytes accessed | tf_op | source)
XLA Modules:
  0.0 68.5 jit_solution(8406479972138202109)
XLA Ops:
  1.9 0.0 copy-start
  1.9 1.0 %copy-done = f32[16,16,512]{2,1,0:T(8,128)S(1)} copy-done((f32[16,16,512]{2,1,0:T(8,128)S(1)}, f32[16,16,512]{2,1,0:T(8,128)}, u32[]{:S(2)}) %copy-start) | copy-done | bytes 524312
  3.0 62.9 %moments.1 = (f32[8,16,16,512]{3,2,1,0:T(8,128)S(1)}, f32[8,8]{1,0:T(8,128)S(1)}) custom-call(f32[8,16,16,512]{3,2,1,0:T(8,128)} %probes_hbm.1, f32[16,16,512]{2,1,0:T(8,128)S(1)} %copy-done, f32[1]{0:T(128)S(6)} %copy.9.center, f32[1]{0:T(128)S(6)} %copy.10.width), custom_call_target="tpu_custom_call" | custom-call | tf_op jit(solution)/shard_map/moments/pallas_call | solution.py:208
  65.9 2.0 %copy.8 = f32[8,16,16,512]{3,2,1,0:T(8,128)} copy(f32[8,16,16,512]{3,2,1,0:T(8,128)S(1)} %get-tuple-element.2) | data formatting | bytes 8388608
  67.9 0.6 copy.11
Async XLA Ops:
  1.9 1.0 %copy-start = (f32[16,16,512]{2,1,0:T(8,128)S(1)}, f32[16,16,512]{2,1,0:T(8,128)}, u32[]{:S(2)}) copy-start(f32[16,16,512]{2,1,0:T(8,128)} %disorder_hbm.1) | copy-start | bytes 1572868
where the time goes:
time: 68.6 us; the launch traced here: 68.5 us
  Pallas kernels  62.9 us (92%)
  local copies, waits for them, and re-layouts  3.64 us (5%)
  between operations  1.94 us (3%)
    pallas_call x1, Pallas kernels, local(): pl.pallas_call(functools.partial(kernel, counts, sites), out_shape=(pltpu...  62.9 us
    unnamed x4, local copies, waits for them, and re-layouts  3.64 us

commit v1 on v0

v1 whole, which is shorter than its diff:
```python
import functools

import jax
import jax.numpy as jnp
from jax import lax
from jax.experimental import pallas as pl
from jax.experimental.pallas import tpu as pltpu
from jax.sharding import PartitionSpec as P

STEPS = 4
MESH = pl.DeviceIdType.MESH
ROWS = 8
LEAD = 2
GATE = 4
SPLIT = 2


def kernel(counts, sites, probes_hbm, disorder_hbm, center, width, last, moments, *scratch):
    fields = scratch[:STEPS]
    (disorder, near, faces, coef, acc, gather_x, gather_y, load_sem, face_sem, energy_sem, up_sem, down_sem,
     xs_sem, ys_sem, xr_sem, yr_sem, hr_sem, gxs_sem, gxr_sem, gys_sem, gyr_sem) = scratch[STEPS:]
    n_probes, nx, ny, nz = probes_hbm.shape
    tiles = ny // ROWS
    count_x, count_y = counts
    me_x = lax.axis_index("gx")
    me_y = lax.axis_index("gy")

    top = count_x - 1

    def at_x(offset):
        return (lax.rem(me_x + offset, count_x), me_y)

    def at_y(offset):
        return (me_x, lax.rem(me_y + offset, count_y))

    def load_face(row):
        return pltpu.make_async_copy(
            probes_hbm.at[:, pl.ds(row, 1)], fields[0].at[:, pl.ds(row + 1, 1)], face_sem)

    def load(p):
        return pltpu.make_async_copy(
            probes_hbm.at[p, pl.ds(1, nx - 2)], fields[0].at[p, pl.ds(2, nx - 2)], load_sem)

    def arrived(ref, sem):
        pltpu.make_async_copy(ref, ref, sem).wait()

    def to_high(s, p):
        final_step = s + 1 == STEPS
        return pltpu.make_async_remote_copy(
            fields[s].at[p, 1], fields[s].at[p, nx + 1], xs_sem.at[s],
            hr_sem.at[p] if final_step else xr_sem.at[s % 2, p], device_id=at_x(count_x - 1), device_id_type=MESH)

    def to_low(s, p):
        return pltpu.make_async_remote_copy(
            fields[s].at[p, nx], fields[s].at[p, 0], xs_sem.at[s], xr_sem.at[s % 2, p],
            device_id=at_x(1), device_id_type=MESH)

    def y_sends(s, p):
        return (
            pltpu.make_async_remote_copy(
                faces.at[s, 0, p], near.at[s, 1, p], ys_sem.at[s], yr_sem.at[s % 2, p],
                device_id=at_y(count_y - 1), device_id_type=MESH),
            pltpu.make_async_remote_copy(
                faces.at[s, 1, p], near.at[s, 0, p], ys_sem.at[s], yr_sem.at[s % 2, p],
                device_id=at_y(1), device_id_type=MESH),
        )

    barrier = pltpu.get_barrier_semaphore()

    @pl.when(me_x < top)
    def _():
        pl.semaphore_signal(barrier, inc=1, device_id=(me_x + 1, me_y), device_id_type=MESH)

    @pl.when(me_x > 0)
    def _():
        pl.semaphore_signal(barrier, inc=1, device_id=(me_x - 1, me_y), device_id_type=MESH)

    for offset in range(1, count_y):
        pl.semaphore_signal(barrier, inc=1, device_id=at_y(offset), device_id_type=MESH)

    for row in (0, nx - 1):
        load_face(row).start()

    @pl.loop(0, n_probes)
    def _(p):
        load(p).start()

    energy = pltpu.make_async_copy(disorder_hbm, disorder, energy_sem)
    energy.start()

    arrived(fields[0].at[:, pl.ds(0, 2)], face_sem)
    pl.semaphore_wait(barrier, count_y - 1 + (me_x < top).astype(jnp.int32) + (me_x > 0).astype(jnp.int32))

    if count_x > 2:
        @pl.when(me_x == 1)
        def _():
            pl.semaphore_signal(up_sem, inc=1, device_id=(me_x + 1, me_y), device_id_type=MESH)

        @pl.when(me_x == top - 1)
        def _():
            pl.semaphore_signal(down_sem, inc=1, device_id=(me_x - 1, me_y), device_id_type=MESH)

    def adjacent_sends(p):
        @pl.when(me_x < top)
        def _():
            to_low(0, p).start()

        @pl.when(me_x > 0)
        def _():
            to_high(0, p).start()

    def wrapped_sends(p):
        @pl.when(me_x == top)
        def _():
            to_low(0, p).start()

        @pl.when(me_x == 0)
        def _():
            to_high(0, p).start()

    lead = min(LEAD, n_probes)
    pl.loop(0, lead)(adjacent_sends)

    if count_x > 2:
        @pl.when(me_x > 1)
        def _():
            pl.semaphore_wait(up_sem, 1)

            @pl.when(me_x < top)
            def _():
                pl.semaphore_signal(up_sem, inc=1, device_id=(me_x + 1, me_y), device_id_type=MESH)

        @pl.when(me_x < top - 1)
        def _():
            pl.semaphore_wait(down_sem, 1)

            @pl.when(me_x > 0)
            def _():
                pl.semaphore_signal(down_sem, inc=1, device_id=(me_x - 1, me_y), device_id_type=MESH)

    @pl.loop(lead, n_probes)
    def _(p):
        adjacent_sends(p)
        wrapped_sends(p - lead)

    pl.loop(n_probes - lead, n_probes)(wrapped_sends)
    arrived(fields[0].at[:, pl.ds(2, nx - 2)], load_sem)

    @pl.loop(0, n_probes)
    def _(p):
        @pl.loop(0, nx)
        def _(x):
            faces[0, 0, p, x] = fields[0][p, x + 1, pl.ds(0, 1)]
            faces[0, 1, p, x] = fields[0][p, x + 1, pl.ds(ny - 1, 1)]

        for copy in y_sends(0, p):
            copy.start()

    scale = 2.0 / jnp.full((ROWS, nz), width[0], jnp.float32)
    middle = center[0]
    energy.wait()

    @pl.loop(0, nx)
    def _(x):
        for i in range(tiles):
            part = pl.ds(ROWS * i, ROWS)
            coef[x, part] = (disorder[x, part] - middle) * scale

    sub = lax.broadcasted_iota(jnp.int32, (ROWS, nz), 0)
    first = sub == 0
    final = sub == ROWS - 1
    lanes = lax.broadcasted_iota(jnp.int32, (n_probes, 128), 1)
    sums = jnp.zeros((n_probes, 128), jnp.float32)

    def fold(v):
        parts = [v[:, 128 * j:128 * (j + 1)] for j in range(nz // 128)]
        while len(parts) > 1:
            parts = [a + b for a, b in zip(parts[::2], parts[1::2])] + (
                [parts[-1]] if len(parts) % 2 else [])
        return parts[0]

    for s in range(STEPS):
        cur = fields[s]
        final_step = s + 1 == STEPS

        @pl.loop(0, n_probes)
        def _(p):
            if final_step:
                to_low(s, p).wait_recv()

                @pl.when(p >= GATE)
                def _():
                    to_high(s, p - GATE).start()
            else:
                arrived(cur.at[p, pl.ds(0, 2)], xr_sem.at[s % 2, p])
            arrived(near.at[s, :, p], yr_sem.at[s % 2, p])

            def row(x, carry, edge=False):
                square, cross = carry
                low = jnp.broadcast_to(near[s, 0, p, x], (ROWS, nz))
                high = jnp.broadcast_to(near[s, 1, p, x], (ROWS, nz))
                here = [cur[p, x + 1, pl.ds(ROWS * i, ROWS)] for i in range(tiles)]
                down = [pltpu.roll(v, 1, 0) for v in here]
                up = [pltpu.roll(v, ROWS - 1, 0) for v in here]
                for i in range(tiles):
                    part = pl.ds(ROWS * i, ROWS)
                    v = here[i]
                    below = jnp.where(first, low if i == 0 else down[i - 1], down[i])
                    above = jnp.where(final, high if i == tiles - 1 else up[i + 1], up[i])
                    beside = cur[p, x, part]
                    if not edge:
                        beside = beside + cur[p, x + 2, part]
                    beside = beside + (below + above)
                    beside = beside + (pltpu.roll(v, 1, 1) + pltpu.roll(v, nz - 1, 1))
                    new = coef[x, part] * v - scale * beside
                    if s == 0:
                        new = 0.5 * new
                    else:
                        new = new - fields[s - 1][p, x + 1, part]
                    if not final_step:
                        fields[s + 1][p, x + 1, part] = new
                        if i == 0:
                            faces[s + 1, 0, p, x] = new[0:1]
                        if i == tiles - 1:
                            faces[s + 1, 1, p, x] = new[ROWS - 1:ROWS]
                    else:
                        last[p, x, part] = new
                    square = square + fold(v * v)
                    cross = cross + fold(new * v)
                return square, cross

            zero = jnp.zeros((ROWS, 128), jnp.float32)
            if final_step:
                square, cross = lax.fori_loop(0, nx - 1, row, (zero, zero), unroll=nx - 1)
                square, cross = row(nx - 1, (square, cross), edge=True)
                for i in range(tiles):
                    part = pl.ds(ROWS * i, ROWS)
                    cross = cross - fold(scale * cur[p, 0, part] * cur[p, 1, part])
            else:
                square, cross = lax.fori_loop(0, nx, row, (zero, zero), unroll=nx)
            acc[0, p] = square
            acc[1, p] = cross
            if s + 1 < STEPS:
                to_low(s + 1, p).start()
                for copy in y_sends(s + 1, p):
                    copy.start()
                if s + 2 < STEPS:
                    to_high(s + 1, p).start()

        for k in range(2):
            total = jnp.sum(jnp.sum(acc[k], axis=1), axis=1, keepdims=True)
            sums = sums + jnp.where(lanes == 2 * s + k, total, 0.0)

    def spread(value, gather, send, recv, me, count, where):
        gather[me] = value
        for offset in range(1, count):
            pltpu.make_async_remote_copy(
                gather.at[me], gather.at[me], send, recv, device_id=where(offset), device_id_type=MESH).start()

    def collect(gather, recv, count):
        arrived(gather.at[pl.ds(0, count - 1)], recv)
        total = gather[0]
        for k in range(1, count):
            total = total + gather[k]
        return total

    def finish(p):
        to_high(STEPS - 1, p).wait_recv()
        for i in range(tiles):
            part = pl.ds(ROWS * i, ROWS)
            last[p, nx - 1, part] = last[p, nx - 1, part] - scale * fields[STEPS - 1][p, nx + 1, part]

    spread(sums, gather_x, gxs_sem, gxr_sem, me_x, count_x, at_x)

    @pl.loop(n_probes - GATE, n_probes)
    def _(p):
        to_high(STEPS - 1, p).start()

    for s in range(STEPS):
        if s + 1 < STEPS:
            arrived(fields[s].at[:, pl.ds(0, 2)], xs_sem.at[s])
        arrived(faces.at[s], ys_sem.at[s])

    pl.loop(0, SPLIT)(finish)
    sums = collect(gather_x, gxr_sem, count_x)
    spread(sums, gather_y, gys_sem, gyr_sem, me_y, count_y, at_y)
    pl.loop(SPLIT, n_probes)(finish)
    sums = collect(gather_y, gyr_sem, count_y)
    mean = sums / jnp.float32(sites)
    start = jnp.where(lax.rem(lanes, 2) == 0, mean[:, 0:1], mean[:, 1:2])
    moments[...] = (2.0 * mean - start)[:, :2 * STEPS]

    arrived(fields[STEPS - 1].at[:, pl.ds(0, 2)], xs_sem.at[STEPS - 1])
    arrived(gather_x.at[pl.ds(0, count_x - 1)], gxs_sem)
    arrived(gather_y.at[pl.ds(0, count_y - 1)], gys_sem)


def local(counts, probes, disorder, spectrum_center, half_width):
    n_probes, nx, ny, nz = probes.shape
    sites = nx * counts[0] * ny * counts[1] * nz
    f32 = jnp.float32
    dma = pltpu.SemaphoreType.DMA
    vmem = pl.BlockSpec(memory_space=pltpu.VMEM)
    smem = pl.BlockSpec(memory_space=pltpu.SMEM)
    hbm = pl.BlockSpec(memory_space=pltpu.HBM)
    return pl.pallas_call(
        functools.partial(kernel, counts, sites),
        out_shape=(
            pltpu.VMEM(probes.shape, f32),
            jax.ShapeDtypeStruct((n_probes, 2 * STEPS), f32),
        ),
        in_specs=[hbm, hbm, smem, smem],
        out_specs=(vmem, vmem),
        scratch_shapes=[pltpu.VMEM((n_probes, nx + 2, ny, nz), f32)] * STEPS + [
            pltpu.VMEM((nx, ny, nz), f32),
            pltpu.VMEM((STEPS, 2, n_probes, nx, 1, nz), f32),
            pltpu.VMEM((STEPS, 2, n_probes, nx, 1, nz), f32),
            pltpu.VMEM((nx, ny, nz), f32),
            pltpu.VMEM((2, n_probes, ROWS, 128), f32),
            pltpu.VMEM((counts[0], n_probes, 128), f32),
            pltpu.VMEM((counts[1], n_probes, 128), f32),
            dma,
            dma,
            dma,
            pltpu.SemaphoreType.REGULAR,
            pltpu.SemaphoreType.REGULAR,
            dma((STEPS,)),
            dma((STEPS,)),
            dma((2, n_probes)),
            dma((2, n_probes)),
            dma((n_probes,)),
            dma,
            dma,
            dma,
            dma,
        ],
        compiler_params=pltpu.CompilerParams(
            collective_id=0, has_side_effects=True, vmem_limit_bytes=46 * 1024 * 1024),
        name="moments",
    )(*(pltpu.with_memory_space_constraint(x, pltpu.HBM) for x in (probes, disorder)),
      spectrum_center, half_width)


def solution(mesh):
    counts = (mesh.shape["gx"], mesh.shape["gy"])
    in_specs = (P(None, "gx", "gy", None), P("gx", "gy", None), P(), P())
    out_specs = (P(None, "gx", "gy", None), P())
    return jax.shard_map(functools.partial(local, counts), mesh=mesh, in_specs=in_specs,
                         out_specs=out_specs, check_vma=False)
```

time: 68.6 us -> 59.2 us (0.86)
  Pallas kernels: 62.9 us -> 54.5 us
  local copies, waits for them, and re-layouts: 3.64 us -> 2.61 us
    pallas_call x1, Pallas kernels: 62.9 us -> 54.5 us  [local(): pl.pallas_call(functools.partial(kernel, counts, sites), out_shape=(pltpu...]
    unnamed x4 -> x2, local copies, waits for them, and re-layouts: 3.64 us -> 2.61 us
where the time goes in v1:
time: 59.2 us; the launch traced here: 59 us
  Pallas kernels  54.5 us (92%)
  local copies, waits for them, and re-layouts  2.61 us (4%)
  between operations  1.93 us (3%)
    pallas_call x1, Pallas kernels, local(): pl.pallas_call(functools.partial(kernel, counts, sites), out_shape=(pltpu...  54.5 us
    unnamed x2, local copies, waits for them, and re-layouts  2.61 us

profile of v1, /device:TPU:0, one launch (start us, length us, event | category | flops | bytes accessed | tf_op | source)
XLA Modules:
  0.0 59.0 jit_solution(14267243624432795804)
XLA Ops:
  1.9 54.5 %moments.1 = (f32[8,16,16,512]{3,2,1,0:T(8,128)S(1)}, f32[8,8]{1,0:T(8,128)S(1)}) custom-call(f32[8,16,16,512]{3,2,1,0:T(8,128)} %probes_hbm.1, f32[16,16,512]{2,1,0:T(8,128)} %disorder_hbm.1, f32[1]{0:T(128)S(6)} %copy.9.center, f32[1]{0:T(128)S(6)} %copy.10.width), custom_call_target="tpu_custom_call" | custom-call | tf_op jit(solution)/shard_map/moments/pallas_call | solution.py:306
  56.4 2.0 %copy.8 = f32[8,16,16,512]{3,2,1,0:T(8,128)} copy(f32[8,16,16,512]{3,2,1,0:T(8,128)S(1)} %get-tuple-element.2) | data formatting | bytes 8388608
  58.4 0.6 %copy.11 = f32[8,8]{1,0:T(8,128)} copy(f32[8,8]{1,0:T(8,128)S(1)} %get-tuple-element.7) | data formatting | bytes 512

commit v2 on v1

--- a/solution.py
+++ b/solution.py
@@ -10,22 +10,31 @@
 STEPS = 4
 MESH = pl.DeviceIdType.MESH
 ROWS = 8
-LEAD = 2
-GATE = 4
+LEAD = (4, 2)
+GATES = (4, 5, 8)
 SPLIT = 2
 
 
 def kernel(counts, sites, probes_hbm, disorder_hbm, center, width, last, moments, *scratch):
     fields = scratch[:STEPS]
     (disorder, near, faces, coef, acc, gather_x, gather_y, load_sem, face_sem, energy_sem, up_sem, down_sem,
-     xs_sem, ys_sem, xr_sem, yr_sem, hr_sem, gxs_sem, gxr_sem, gys_sem, gyr_sem) = scratch[STEPS:]
+     round_sem, xs_sem, ys_sem, recv_sem, high_sem, gxs_sem, gxr_sem, gys_sem, gyr_sem) = scratch[STEPS:]
     n_probes, nx, ny, nz = probes_hbm.shape
     tiles = ny // ROWS
+    assert 2 * nx % ny == 0 and 2 * STEPS <= nx + 2
     count_x, count_y = counts
     me_x = lax.axis_index("gx")
     me_y = lax.axis_index("gy")
 
     top = count_x - 1
+    gate = jnp.where(me_x == 0, GATES[0], jnp.where(me_x == top, GATES[2], GATES[1]))
+    if count_y & (count_y - 1):
+        mates = [lax.rem(me_y + k, count_y) for k in range(1, count_y)]
+        rounds = 0
+    else:
+        widths = [1 << k for k in range(count_y.bit_length() - 1)]
+        mates = [me_y + w * (1 - 2 * lax.rem(lax.div(me_y, w), 2)) for w in widths]
+        rounds = len(widths) - 1
 
     def at_x(offset):
         return (lax.rem(me_x + offset, count_x), me_y)
@@ -47,21 +56,21 @@
     def to_high(s, p):
         final_step = s + 1 == STEPS
         return pltpu.make_async_remote_copy(
-            fields[s].at[p, 1], fields[s].at[p, nx + 1], xs_sem.at[s],
-            hr_sem.at[p] if final_step else xr_sem.at[s % 2, p], device_id=at_x(count_x - 1), device_id_type=MESH)
+            fields[s].at[p, 1], fields[s].at[p, nx + 1], xs_sem,
+            high_sem.at[p] if final_step else recv_sem.at[s % 2, p], device_id=at_x(count_x - 1), device_id_type=MESH)
 
     def to_low(s, p):
         return pltpu.make_async_remote_copy(
-            fields[s].at[p, nx], fields[s].at[p, 0], xs_sem.at[s], xr_sem.at[s % 2, p],
+            fields[s].at[p, nx], fields[s].at[p, 0], xs_sem, recv_sem.at[s % 2, p],
             device_id=at_x(1), device_id_type=MESH)
 
     def y_sends(s, p):
         return (
             pltpu.make_async_remote_copy(
-                faces.at[s, 0, p], near.at[s, 1, p], ys_sem.at[s], yr_sem.at[s % 2, p],
+                faces.at[s, 0, p], near.at[s, 1, p], ys_sem, recv_sem.at[s % 2, p],
                 device_id=at_y(count_y - 1), device_id_type=MESH),
             pltpu.make_async_remote_copy(
-                faces.at[s, 1, p], near.at[s, 0, p], ys_sem.at[s], yr_sem.at[s % 2, p],
+                faces.at[s, 1, p], near.at[s, 0, p], ys_sem, recv_sem.at[s % 2, p],
                 device_id=at_y(1), device_id_type=MESH),
         )
 
@@ -75,8 +84,8 @@
     def _():
         pl.semaphore_signal(barrier, inc=1, device_id=(me_x - 1, me_y), device_id_type=MESH)
 
-    for offset in range(1, count_y):
-        pl.semaphore_signal(barrier, inc=1, device_id=at_y(offset), device_id_type=MESH)
+    for mate in mates:
+        pl.semaphore_signal(barrier, inc=1, device_id=(me_x, mate), device_id_type=MESH)
 
     for row in (0, nx - 1):
         load_face(row).start()
@@ -89,70 +98,98 @@
     energy.start()
 
     arrived(fields[0].at[:, pl.ds(0, 2)], face_sem)
-    pl.semaphore_wait(barrier, count_y - 1 + (me_x < top).astype(jnp.int32) + (me_x > 0).astype(jnp.int32))
-
-    if count_x > 2:
-        @pl.when(me_x == 1)
-        def _():
+    pl.semaphore_wait(barrier, len(mates) + (me_x < top).astype(jnp.int32) + (me_x > 0).astype(jnp.int32))
+
+    def greet(k):
+        for mate in mates:
+            pl.semaphore_signal(round_sem.at[k], inc=1, device_id=(me_x, mate), device_id_type=MESH)
+
+    def take_faces(p):
+        def row(x, carry):
+            faces[0, 0, p, x] = fields[0][p, x + 1, pl.ds(0, 1)]
+            faces[0, 1, p, x] = fields[0][p, x + 1, pl.ds(ny - 1, 1)]
+            return carry
+
+        lax.fori_loop(0, nx, row, 0, unroll=4)
+
+    if rounds:
+        greet(0)
+
+    @pl.when(me_x == 1)
+    def _():
+        if count_x > 2:
             pl.semaphore_signal(up_sem, inc=1, device_id=(me_x + 1, me_y), device_id_type=MESH)
 
-        @pl.when(me_x == top - 1)
-        def _():
+    @pl.when(me_x == top - 1)
+    def _():
+        if count_x > 2:
             pl.semaphore_signal(down_sem, inc=1, device_id=(me_x - 1, me_y), device_id_type=MESH)
 
-    def adjacent_sends(p):
-        @pl.when(me_x < top)
-        def _():
+    lead = [min(k, n_probes) for k in LEAD]
+
+    @pl.when(me_x == 0)
+    def _():
+        for p in range(lead[0]):
             to_low(0, p).start()
 
-        @pl.when(me_x > 0)
-        def _():
+    @pl.when(me_x == top)
+    def _():
+        for p in range(lead[1]):
             to_high(0, p).start()
 
-    def wrapped_sends(p):
-        @pl.when(me_x == top)
-        def _():
+    @pl.when(jnp.logical_and(me_x > 0, me_x < top))
+    def _():
+        @pl.loop(0, n_probes)
+        def _(p):
             to_low(0, p).start()
-
-        @pl.when(me_x == 0)
-        def _():
             to_high(0, p).start()
 
-    lead = min(LEAD, n_probes)
-    pl.loop(0, lead)(adjacent_sends)
-
-    if count_x > 2:
+    arrived(fields[0].at[:, pl.ds(2, nx - 2)], load_sem)
+    half = n_probes // 2
+    pl.loop(0, half)(take_faces)
+
+    @pl.when(jnp.logical_and(me_x > 0, me_x < top))
+    def _():
         @pl.when(me_x > 1)
         def _():
             pl.semaphore_wait(up_sem, 1)
-
-            @pl.when(me_x < top)
-            def _():
-                pl.semaphore_signal(up_sem, inc=1, device_id=(me_x + 1, me_y), device_id_type=MESH)
+            pl.semaphore_signal(up_sem, inc=1, device_id=(me_x + 1, me_y), device_id_type=MESH)
 
         @pl.when(me_x < top - 1)
         def _():
             pl.semaphore_wait(down_sem, 1)
-
-            @pl.when(me_x > 0)
-            def _():
-                pl.semaphore_signal(down_sem, inc=1, device_id=(me_x - 1, me_y), device_id_type=MESH)
-
-    @pl.loop(lead, n_probes)
+            pl.semaphore_signal(down_sem, inc=1, device_id=(me_x - 1, me_y), device_id_type=MESH)
+
+    for k in range(rounds):
+        pl.semaphore_wait(round_sem.at[k], len(mates))
+        if k + 1 < rounds:
+            greet(k + 1)
+
+    @pl.loop(0, half)
     def _(p):
-        adjacent_sends(p)
-        wrapped_sends(p - lead)
-
-    pl.loop(n_probes - lead, n_probes)(wrapped_sends)
-    arrived(fields[0].at[:, pl.ds(2, nx - 2)], load_sem)
-
-    @pl.loop(0, n_probes)
+        for copy in y_sends(0, p):
+            copy.start()
+
+    def other_sends(lead, adjacent, wrapped, proof):
+        if count_x > 2:
+            pl.semaphore_wait(proof, 1)
+        for p in range(lead, n_probes):
+            wrapped(0, p - lead).start()
+            adjacent(0, p).start()
+        for p in range(n_probes - lead, n_probes):
+            wrapped(0, p).start()
+
+    @pl.when(me_x == 0)
+    def _():
+        other_sends(lead[0], to_low, to_high, down_sem)
+
+    @pl.when(me_x == top)
+    def _():
+        other_sends(lead[1], to_high, to_low, up_sem)
+
+    @pl.loop(half, n_probes)
     def _(p):
-        @pl.loop(0, nx)
-        def _(x):
-            faces[0, 0, p, x] = fields[0][p, x + 1, pl.ds(0, 1)]
-            faces[0, 1, p, x] = fields[0][p, x + 1, pl.ds(ny - 1, 1)]
-
+        take_faces(p)
         for copy in y_sends(0, p):
             copy.start()
 
@@ -185,15 +222,11 @@
 
         @pl.loop(0, n_probes)
         def _(p):
+            arrived(cur.at[p, pl.ds(0, 2 * nx // ny + (1 if final_step else 2))], recv_sem.at[s % 2, p])
             if final_step:
-                to_low(s, p).wait_recv()
-
-                @pl.when(p >= GATE)
+                @pl.when(p >= gate)
                 def _():
-                    to_high(s, p - GATE).start()
-            else:
-                arrived(cur.at[p, pl.ds(0, 2)], xr_sem.at[s % 2, p])
-            arrived(near.at[s, :, p], yr_sem.at[s % 2, p])
+                    to_high(s, p - gate).start()
 
             def row(x, carry, edge=False):
                 square, cross = carry
@@ -272,14 +305,9 @@
 
     spread(sums, gather_x, gxs_sem, gxr_sem, me_x, count_x, at_x)
 
-    @pl.loop(n_probes - GATE, n_probes)
+    @pl.loop(n_probes - gate, n_probes)
     def _(p):
         to_high(STEPS - 1, p).start()
-
-    for s in range(STEPS):
-        if s + 1 < STEPS:
-            arrived(fields[s].at[:, pl.ds(0, 2)], xs_sem.at[s])
-        arrived(faces.at[s], ys_sem.at[s])
 
     pl.loop(0, SPLIT)(finish)
     sums = collect(gather_x, gxr_sem, count_x)
@@ -290,9 +318,19 @@
     start = jnp.where(lax.rem(lanes, 2) == 0, mean[:, 0:1], mean[:, 1:2])
     moments[...] = (2.0 * mean - start)[:, :2 * STEPS]
 
-    arrived(fields[STEPS - 1].at[:, pl.ds(0, 2)], xs_sem.at[STEPS - 1])
+    arrived(fields[0].at[:, pl.ds(0, 2 * STEPS)], xs_sem)
+    arrived(faces, ys_sem)
     arrived(gather_x.at[pl.ds(0, count_x - 1)], gxs_sem)
     arrived(gather_y.at[pl.ds(0, count_y - 1)], gys_sem)
+
+
+def write_out(last, moments, last_hbm, moments_hbm, last_sem, moments_sem):
+    small = pltpu.make_async_copy(moments, moments_hbm, moments_sem)
+    small.start()
+    for p in range(last.shape[0]):
+        pltpu.make_async_copy(last.at[p], last_hbm.at[p], last_sem).start()
+    small.wait()
+    pltpu.make_async_copy(last, last_hbm, last_sem).wait()
 
 
 def local(counts, probes, disorder, spectrum_center, half_width):
@@ -303,7 +341,7 @@
     vmem = pl.BlockSpec(memory_space=pltpu.VMEM)
     smem = pl.BlockSpec(memory_space=pltpu.SMEM)
     hbm = pl.BlockSpec(memory_space=pltpu.HBM)
-    return pl.pallas_call(
+    held = pl.pallas_call(
         functools.partial(kernel, counts, sites),
         out_shape=(
             pltpu.VMEM(probes.shape, f32),
@@ -324,9 +362,9 @@
             dma,
             pltpu.SemaphoreType.REGULAR,
             pltpu.SemaphoreType.REGULAR,
-            dma((STEPS,)),
-            dma((STEPS,)),
-            dma((2, n_probes)),
+            pltpu.SemaphoreType.REGULAR((max(counts[1].bit_length() - 2, 1),)),
+            dma,
+            dma,
             dma((2, n_probes)),
             dma((n_probes,)),
             dma,
@@ -335,10 +373,19 @@
             dma,
         ],
         compiler_params=pltpu.CompilerParams(
-            collective_id=0, has_side_effects=True, vmem_limit_bytes=46 * 1024 * 1024),
+            collective_id=0, has_side_effects=True, vmem_limit_bytes=32 * 1024 * 1024),
         name="moments",
     )(*(pltpu.with_memory_space_constraint(x, pltpu.HBM) for x in (probes, disorder)),
       spectrum_center, half_width)
+    return pl.pallas_call(
+        write_out,
+        out_shape=(jax.ShapeDtypeStruct(probes.shape, f32), jax.ShapeDtypeStruct((n_probes, 2 * STEPS), f32)),
+        in_specs=[vmem] * 2,
+        out_specs=(hbm,) * 2,
+        scratch_shapes=[dma, dma],
+        compiler_params=pltpu.CompilerParams(vmem_limit_bytes=8 * 1024 * 1024),
+        name="write_out",
+    )(*(pltpu.with_memory_space_constraint(x, pltpu.VMEM) for x in held))
 
 
 def solution(mesh):

time: 59.2 us -> 57.8 us (0.976)
  local copies, waits for them, and re-layouts: 2.61 us -> 0 us
  Pallas kernels: 54.5 us -> 55.7 us
    unnamed x2 -> x0, local copies, waits for them, and re-layouts: 2.61 us -> none
    pallas_call x0 -> x1, Pallas kernels: none -> 2.02 us  [local(): pl.pallas_call(write_out, out_shape=(jax.ShapeDtypeStruct(probes.shape, f...]
    pallas_call x1, Pallas kernels: 54.5 us -> 53.7 us  [local(): pl.pallas_call(functools.partial(kernel, counts, sites), out_shape=(pltpu...]
where the time goes in v2:
time: 57.8 us; the launch traced here: 57.6 us
  Pallas kernels  55.7 us (96%)
  between operations  1.93 us (3%)
    pallas_call x1, Pallas kernels, local(): pl.pallas_call(functools.partial(kernel, counts, sites), out_shape=(pltpu...  53.7 us
    pallas_call x1, Pallas kernels, local(): pl.pallas_call(write_out, out_shape=(jax.ShapeDtypeStruct(probes.shape, f...  2.02 us

profile of v2, /device:TPU:0, one launch (start us, length us, event | category | flops | bytes accessed | tf_op | source)
XLA Modules:
  0.0 57.6 jit_solution(2878844883667202484)
XLA Ops:
  1.9 53.7 %moments.1 = (f32[8,16,16,512]{3,2,1,0:T(8,128)S(1)}, f32[8,8]{1,0:T(8,128)S(1)}) custom-call(f32[8,16,16,512]{3,2,1,0:T(8,128)} %probes_hbm.1, f32[16,16,512]{2,1,0:T(8,128)} %disorder_hbm.1, f32[1]{0:T(128)S(6)} %copy.6.center, f32[1]{0:T(128)S(6)} %copy.7.width), custom_call_target="tpu_custom_call" | custom-call | tf_op jit(solution)/shard_map/moments/pallas_call | solution.py:344
  55.6 2.0 %write_out.1 = (f32[8,16,16,512]{3,2,1,0:T(8,128)}, f32[8,8]{1,0:T(8,128)}) custom-call(f32[8,16,16,512]{3,2,1,0:T(8,128)S(1)} %get-tuple-element.4.last, f32[8,8]{1,0:T(8,128)S(1)} %get-tuple-element.5.moments), custom_call_target="tpu_custom_call" | custom-call | tf_op jit(solution)/shard_map/write_out/pallas_call | solution.py:380

commit v3 on v2

--- a/solution.py
+++ b/solution.py
@@ -10,8 +10,8 @@
 STEPS = 4
 MESH = pl.DeviceIdType.MESH
 ROWS = 8
-LEAD = (4, 2)
-GATES = (4, 5, 8)
+LEAD = (5, 4)
+GATES = (4, 5, 6, 8)
 SPLIT = 2
 
 
@@ -27,7 +27,7 @@
     me_y = lax.axis_index("gy")
 
     top = count_x - 1
-    gate = jnp.where(me_x == 0, GATES[0], jnp.where(me_x == top, GATES[2], GATES[1]))
+    gate = jnp.where(me_x == 0, GATES[0], jnp.where(me_x == 1, GATES[1], jnp.where(me_x < top, GATES[2], GATES[3])))
     if count_y & (count_y - 1):
         mates = [lax.rem(me_y + k, count_y) for k in range(1, count_y)]
         rounds = 0
@@ -145,30 +145,7 @@
             to_high(0, p).start()
 
     arrived(fields[0].at[:, pl.ds(2, nx - 2)], load_sem)
-    half = n_probes // 2
-    pl.loop(0, half)(take_faces)
-
-    @pl.when(jnp.logical_and(me_x > 0, me_x < top))
-    def _():
-        @pl.when(me_x > 1)
-        def _():
-            pl.semaphore_wait(up_sem, 1)
-            pl.semaphore_signal(up_sem, inc=1, device_id=(me_x + 1, me_y), device_id_type=MESH)
-
-        @pl.when(me_x < top - 1)
-        def _():
-            pl.semaphore_wait(down_sem, 1)
-            pl.semaphore_signal(down_sem, inc=1, device_id=(me_x - 1, me_y), device_id_type=MESH)
-
-    for k in range(rounds):
-        pl.semaphore_wait(round_sem.at[k], len(mates))
-        if k + 1 < rounds:
-            greet(k + 1)
-
-    @pl.loop(0, half)
-    def _(p):
-        for copy in y_sends(0, p):
-            copy.start()
+    pl.loop(0, n_probes)(take_faces)
 
     def other_sends(lead, adjacent, wrapped, proof):
         if count_x > 2:
@@ -179,17 +156,36 @@
         for p in range(n_probes - lead, n_probes):
             wrapped(0, p).start()
 
-    @pl.when(me_x == 0)
-    def _():
-        other_sends(lead[0], to_low, to_high, down_sem)
-
-    @pl.when(me_x == top)
-    def _():
-        other_sends(lead[1], to_high, to_low, up_sem)
-
-    @pl.loop(half, n_probes)
+    def pass_on():
+        @pl.when(jnp.logical_and(me_x > 1, me_x < top))
+        def _():
+            pl.semaphore_wait(up_sem, 1)
+            pl.semaphore_signal(up_sem, inc=1, device_id=(me_x + 1, me_y), device_id_type=MESH)
+
+        @pl.when(jnp.logical_and(me_x > 0, me_x < top - 1))
+        def _():
+            pl.semaphore_wait(down_sem, 1)
+            pl.semaphore_signal(down_sem, inc=1, device_id=(me_x - 1, me_y), device_id_type=MESH)
+
+        @pl.when(me_x == 0)
+        def _():
+            other_sends(lead[0], to_low, to_high, down_sem)
+
+        @pl.when(me_x == top)
+        def _():
+            other_sends(lead[1], to_high, to_low, up_sem)
+
+    for k in range(rounds):
+        pl.semaphore_wait(round_sem.at[k], len(mates))
+        if k + 1 < rounds:
+            greet(k + 1)
+        if k == 0:
+            pass_on()
+    if not rounds:
+        pass_on()
+
+    @pl.loop(0, n_probes)
     def _(p):
-        take_faces(p)
         for copy in y_sends(0, p):
             copy.start()
 

time: 57.8 us -> 57.6 us (level)
  no operation moved by 1% of the time
where the time goes in v3:
time: 57.6 us; the launch traced here: 57.4 us
  Pallas kernels  55.5 us (96%)
  between operations  1.93 us (3%)
    pallas_call x1, Pallas kernels, local(): pl.pallas_call(functools.partial(kernel, counts, sites), out_shape=(pltpu...  53.5 us
    pallas_call x1, Pallas kernels, local(): pl.pallas_call(write_out, out_shape=(jax.ShapeDtypeStruct(probes.shape, f...  2.02 us

profile of v3, /device:TPU:0, one launch (start us, length us, event | category | flops | bytes accessed | tf_op | source)
XLA Modules:
  0.0 57.4 jit_solution(5910738529229837941)
XLA Ops:
  1.9 53.5 %moments.1 = (f32[8,16,16,512]{3,2,1,0:T(8,128)S(1)}, f32[8,8]{1,0:T(8,128)S(1)}) custom-call(f32[8,16,16,512]{3,2,1,0:T(8,128)} %probes_hbm.1, f32[16,16,512]{2,1,0:T(8,128)} %disorder_hbm.1, f32[1]{0:T(128)S(6)} %copy.6.center, f32[1]{0:T(128)S(6)} %copy.7.width), custom_call_target="tpu_custom_call" | custom-call | tf_op jit(solution)/shard_map/moments/pallas_call | solution.py:340
  55.4 2.0 %write_out.1 = (f32[8,16,16,512]{3,2,1,0:T(8,128)}, f32[8,8]{1,0:T(8,128)}) custom-call(f32[8,16,16,512]{3,2,1,0:T(8,128)S(1)} %get-tuple-element.4.last, f32[8,8]{1,0:T(8,128)S(1)} %get-tuple-element.5.moments), custom_call_target="tpu_custom_call" | custom-call | tf_op jit(solution)/shard_map/write_out/pallas_call | solution.py:376

commit v4 on v3

--- a/solution.py
+++ b/solution.py
@@ -18,10 +18,10 @@
 def kernel(counts, sites, probes_hbm, disorder_hbm, center, width, last, moments, *scratch):
     fields = scratch[:STEPS]
     (disorder, near, faces, coef, acc, gather_x, gather_y, load_sem, face_sem, energy_sem, up_sem, down_sem,
-     round_sem, xs_sem, ys_sem, recv_sem, high_sem, gxs_sem, gxr_sem, gys_sem, gyr_sem) = scratch[STEPS:]
+     round_sem, xs_sem, ys_sem, recv_sem, low_sem, high_sem, gxs_sem, gxr_sem, gys_sem, gyr_sem) = scratch[STEPS:]
     n_probes, nx, ny, nz = probes_hbm.shape
     tiles = ny // ROWS
-    assert 2 * nx % ny == 0 and 2 * STEPS <= nx + 2
+    assert 2 * nx % ny == 0 and 2 * STEPS <= nx + 2 and 2 * STEPS * n_probes <= 128
     count_x, count_y = counts
     me_x = lax.axis_index("gx")
     me_y = lax.axis_index("gy")
@@ -61,8 +61,8 @@
 
     def to_low(s, p):
         return pltpu.make_async_remote_copy(
-            fields[s].at[p, nx], fields[s].at[p, 0], xs_sem, recv_sem.at[s % 2, p],
-            device_id=at_x(1), device_id_type=MESH)
+            fields[s].at[p, nx], fields[s].at[p, 0], xs_sem,
+            low_sem.at[p] if s + 1 == STEPS else recv_sem.at[s % 2, p], device_id=at_x(1), device_id_type=MESH)
 
     def y_sends(s, p):
         return (
@@ -203,6 +203,7 @@
     first = sub == 0
     final = sub == ROWS - 1
     lanes = lax.broadcasted_iota(jnp.int32, (n_probes, 128), 1)
+    which = lax.broadcasted_iota(jnp.int32, (n_probes, 128), 0)
     sums = jnp.zeros((n_probes, 128), jnp.float32)
 
     def fold(v):
@@ -218,13 +219,12 @@
 
         @pl.loop(0, n_probes)
         def _(p):
-            arrived(cur.at[p, pl.ds(0, 2 * nx // ny + (1 if final_step else 2))], recv_sem.at[s % 2, p])
             if final_step:
-                @pl.when(p >= gate)
-                def _():
-                    to_high(s, p - gate).start()
-
-            def row(x, carry, edge=False):
+                arrived(near.at[s, :, p], recv_sem.at[s % 2, p])
+            else:
+                arrived(cur.at[p, pl.ds(0, 2 * nx // ny + 2)], recv_sem.at[s % 2, p])
+
+            def row(x, carry, below_x=True, above_x=True):
                 square, cross = carry
                 low = jnp.broadcast_to(near[s, 0, p, x], (ROWS, nz))
                 high = jnp.broadcast_to(near[s, 1, p, x], (ROWS, nz))
@@ -236,10 +236,11 @@
                     v = here[i]
                     below = jnp.where(first, low if i == 0 else down[i - 1], down[i])
                     above = jnp.where(final, high if i == tiles - 1 else up[i + 1], up[i])
-                    beside = cur[p, x, part]
-                    if not edge:
+                    beside = below + above
+                    if below_x:
+                        beside = beside + cur[p, x, part]
+                    if above_x:
                         beside = beside + cur[p, x + 2, part]
-                    beside = beside + (below + above)
                     beside = beside + (pltpu.roll(v, 1, 1) + pltpu.roll(v, nz - 1, 1))
                     new = coef[x, part] * v - scale * beside
                     if s == 0:
@@ -260,11 +261,9 @@
 
             zero = jnp.zeros((ROWS, 128), jnp.float32)
             if final_step:
-                square, cross = lax.fori_loop(0, nx - 1, row, (zero, zero), unroll=nx - 1)
-                square, cross = row(nx - 1, (square, cross), edge=True)
-                for i in range(tiles):
-                    part = pl.ds(ROWS * i, ROWS)
-                    cross = cross - fold(scale * cur[p, 0, part] * cur[p, 1, part])
+                sums_p = row(0, (zero, zero), below_x=False)
+                sums_p = lax.fori_loop(1, nx - 1, row, sums_p, unroll=nx - 2)
+                square, cross = row(nx - 1, sums_p, above_x=False)
             else:
                 square, cross = lax.fori_loop(0, nx, row, (zero, zero), unroll=nx)
             acc[0, p] = square
@@ -276,9 +275,26 @@
                 if s + 2 < STEPS:
                     to_high(s + 1, p).start()
 
+        if final_step:
+            @pl.loop(0, n_probes)
+            def _(p):
+                to_low(s, p).wait_recv()
+
+                @pl.when(p >= gate)
+                def _():
+                    to_high(s, p - gate).start()
+
+                bond = jnp.zeros((ROWS, 128), jnp.float32)
+                for i in range(tiles):
+                    part = pl.ds(ROWS * i, ROWS)
+                    below = scale * cur[p, 0, part]
+                    last[p, 0, part] = last[p, 0, part] - below
+                    bond = bond + fold(below * cur[p, 1, part])
+                acc[1, p] = acc[1, p] - 2.0 * bond
+
         for k in range(2):
             total = jnp.sum(jnp.sum(acc[k], axis=1), axis=1, keepdims=True)
-            sums = sums + jnp.where(lanes == 2 * s + k, total, 0.0)
+            sums = sums + jnp.where(lanes == 2 * (STEPS * which + s) + k, total, 0.0)
 
     def spread(value, gather, send, recv, me, count, where):
         gather[me] = value
@@ -299,6 +315,7 @@
             part = pl.ds(ROWS * i, ROWS)
             last[p, nx - 1, part] = last[p, nx - 1, part] - scale * fields[STEPS - 1][p, nx + 1, part]
 
+    sums = jnp.sum(sums, axis=0, keepdims=True)
     spread(sums, gather_x, gxs_sem, gxr_sem, me_x, count_x, at_x)
 
     @pl.loop(n_probes - gate, n_probes)
@@ -310,7 +327,11 @@
     spread(sums, gather_y, gys_sem, gyr_sem, me_y, count_y, at_y)
     pl.loop(SPLIT, n_probes)(finish)
     sums = collect(gather_y, gyr_sem, count_y)
-    mean = sums / jnp.float32(sites)
+    sums = jnp.broadcast_to(sums, (n_probes, 128))
+    own = sums
+    for p in range(1, n_probes):
+        own = jnp.where(which == p, pltpu.roll(sums, 128 - 2 * STEPS * p, 1), own)
+    mean = own / jnp.float32(sites)
     start = jnp.where(lax.rem(lanes, 2) == 0, mean[:, 0:1], mean[:, 1:2])
     moments[...] = (2.0 * mean - start)[:, :2 * STEPS]
 
@@ -351,8 +372,8 @@
             pltpu.VMEM((STEPS, 2, n_probes, nx, 1, nz), f32),
             pltpu.VMEM((nx, ny, nz), f32),
             pltpu.VMEM((2, n_probes, ROWS, 128), f32),
-            pltpu.VMEM((counts[0], n_probes, 128), f32),
-            pltpu.VMEM((counts[1], n_probes, 128), f32),
+            pltpu.VMEM((counts[0], 1, 128), f32),
+            pltpu.VMEM((counts[1], 1, 128), f32),
             dma,
             dma,
             dma,
@@ -362,6 +383,7 @@
             dma,
             dma,
             dma((2, n_probes)),
+            dma((n_probes,)),
             dma((n_probes,)),
             dma,
             dma,

time: 57.6 us -> 57.3 us (level)
  no operation moved by 1% of the time
where the time goes in v4:
time: 57.3 us; the launch traced here: 57.1 us
  Pallas kernels  55.2 us (96%)
  between operations  1.93 us (3%)
    pallas_call x1, Pallas kernels, local(): pl.pallas_call(functools.partial(kernel, counts, sites), out_shape=(pltpu...  53.1 us
    pallas_call x1, Pallas kernels, local(): pl.pallas_call(write_out, out_shape=(jax.ShapeDtypeStruct(probes.shape, f...  2.02 us

profile of v4, /device:TPU:0, one launch (start us, length us, event | category | flops | bytes accessed | tf_op | source)
XLA Modules:
  0.0 57.1 jit_solution(14269585568918133099)
XLA Ops:
  1.9 53.1 %moments.1 = (f32[8,16,16,512]{3,2,1,0:T(8,128)S(1)}, f32[8,8]{1,0:T(8,128)S(1)}) custom-call(f32[8,16,16,512]{3,2,1,0:T(8,128)} %probes_hbm.1, f32[16,16,512]{2,1,0:T(8,128)} %disorder_hbm.1, f32[1]{0:T(128)S(6)} %copy.6.center, f32[1]{0:T(128)S(6)} %copy.7.width), custom_call_target="tpu_custom_call" | custom-call | tf_op jit(solution)/shard_map/moments/pallas_call | solution.py:361
  55.1 2.0 %write_out.1 = (f32[8,16,16,512]{3,2,1,0:T(8,128)}, f32[8,8]{1,0:T(8,128)}) custom-call(f32[8,16,16,512]{3,2,1,0:T(8,128)S(1)} %get-tuple-element.4.last, f32[8,8]{1,0:T(8,128)S(1)} %get-tuple-element.5.moments), custom_call_target="tpu_custom_call" | custom-call | tf_op jit(solution)/shard_map/write_out/pallas_call | solution.py:398

commit v5 on v4

--- a/solution.py
+++ b/solution.py
@@ -11,7 +11,7 @@
 MESH = pl.DeviceIdType.MESH
 ROWS = 8
 LEAD = (5, 4)
-GATES = (4, 5, 6, 8)
+GATES = (5, 6, 7, 8)
 SPLIT = 2
 
 

time: 57.3 us -> 57.2 us (level)
  no operation moved by 1% of the time
where the time goes in v5:
time: 57.2 us; the launch traced here: 57 us
  Pallas kernels  55.1 us (96%)
  between operations  1.93 us (3%)
    pallas_call x1, Pallas kernels, local(): pl.pallas_call(functools.partial(kernel, counts, sites), out_shape=(pltpu...  53.1 us
    pallas_call x1, Pallas kernels, local(): pl.pallas_call(write_out, out_shape=(jax.ShapeDtypeStruct(probes.shape, f...  2.02 us

profile of v5, /device:TPU:0, one launch (start us, length us, event | category | flops | bytes accessed | tf_op | source)
XLA Modules:
  0.0 57.0 jit_solution(14217917728784424886)
XLA Ops:
  1.9 53.1 %moments.1 = (f32[8,16,16,512]{3,2,1,0:T(8,128)S(1)}, f32[8,8]{1,0:T(8,128)S(1)}) custom-call(f32[8,16,16,512]{3,2,1,0:T(8,128)} %probes_hbm.1, f32[16,16,512]{2,1,0:T(8,128)} %disorder_hbm.1, f32[1]{0:T(128)S(6)} %copy.6.center, f32[1]{0:T(128)S(6)} %copy.7.width), custom_call_target="tpu_custom_call" | custom-call | tf_op jit(solution)/shard_map/moments/pallas_call | solution.py:361
  55.0 2.0 %write_out.1 = (f32[8,16,16,512]{3,2,1,0:T(8,128)}, f32[8,8]{1,0:T(8,128)}) custom-call(f32[8,16,16,512]{3,2,1,0:T(8,128)S(1)} %get-tuple-element.4.last, f32[8,8]{1,0:T(8,128)S(1)} %get-tuple-element.5.moments), custom_call_target="tpu_custom_call" | custom-call | tf_op jit(solution)/shard_map/write_out/pallas_call | solution.py:398
